TPU v7x, 32 devices: a whole 2x2x4 slice. The times are simulated.
32 devices in a mesh: data: 32 (over z, y, x, core).
Axes of the slice: x: 2, y: 2, z: 4, core: 2. Of those that a mesh axis runs over, the one named last changes fastest.
Arguments:
- x_step: bfloat16 [2, 64, 576, 768], P(None, 'data')
- labels: int32 [2, 64], P(None, 'data')
- x_next: bfloat16 [64, 576, 768], P('data')
- w_in: float32 [4, 768, 3072], replicated
- w_out: float32 [4, 3072, 768], replicated
- w_head: float32 [768, 1000], replicated
- mom_in: float32 [4, 768, 3072], replicated
- mom_out: float32 [4, 3072, 768], replicated
- mom_head: float32 [768, 1000], replicated
- learn_rate: float32 [], replicated
- mom_coef: float32 [], replicated
Outputs:
- output 1: float32 [64, 1000], P('data')
- output 2: float32 [4, 768, 3072], replicated
- output 3: float32 [4, 3072, 768], replicated
- output 4: float32 [768, 1000], replicated
- output 5: float32 [4, 768, 3072], replicated
- output 6: float32 [4, 3072, 768], replicated
- output 7: float32 [768, 1000], replicated
All inputs are finite; a program needn't handle non-finite values.
Results may differ from a plain program's by a relative error of at most 0.0167193.
Values are sent between devices in bfloat16 or wider.
A program may use at most 1.25 GiB of HBM per device.

v0:
```python
import jax
import jax.numpy as jnp
from jax import lax
from jax.sharding import PartitionSpec as P

LN_EPS = 1e-6


def norm_rows(x_f32):
    row_mean = jnp.mean(x_f32, axis=-1, keepdims=True)
    centered = x_f32 - row_mean
    row_var = jnp.mean(centered * centered, axis=-1, keepdims=True)
    return centered * lax.rsqrt(row_var + LN_EPS)


def block_forward(tok_act, w_one, w_two):
    x_f32 = tok_act.astype(jnp.float32)
    normed = norm_rows(x_f32).astype(jnp.bfloat16)
    pre_act = jnp.einsum('bsd,df->bsf', normed, w_one, preferred_element_type=jnp.float32)
    hidden = jax.nn.gelu(pre_act).astype(jnp.bfloat16)
    mlp_out = jnp.einsum('bsf,fd->bsd', hidden, w_two, preferred_element_type=jnp.float32)
    return (x_f32 + mlp_out).astype(jnp.bfloat16), (normed, pre_act, hidden)


def block_backward(tok_act, saved_act, d_out, w_one, w_two, need_input):
    normed, pre_act, hidden = saved_act
    d_out_b = d_out.astype(jnp.bfloat16)
    g_two = jnp.einsum('bsf,bsd->fd', hidden, d_out_b, preferred_element_type=jnp.float32)
    d_hidden = jnp.einsum('bsd,fd->bsf', d_out_b, w_two, preferred_element_type=jnp.float32)
    _, gelu_back = jax.vjp(jax.nn.gelu, pre_act)
    d_pre = gelu_back(d_hidden)[0].astype(jnp.bfloat16)
    g_one = jnp.einsum('bsd,bsf->df', normed, d_pre, preferred_element_type=jnp.float32)
    if not need_input:
        return g_one, g_two, d_out
    d_normed = jnp.einsum('bsf,df->bsd', d_pre, w_one, preferred_element_type=jnp.float32)
    _, norm_back = jax.vjp(norm_rows, tok_act.astype(jnp.float32))
    return g_one, g_two, d_out + norm_back(d_normed)[0]


def head_logits(tok_act, w_head_b):
    pooled = jnp.mean(tok_act, axis=1, dtype=jnp.float32).astype(jnp.bfloat16)
    return pooled, jnp.dot(pooled, w_head_b, preferred_element_type=jnp.float32)


def head_backward(tok_act, lab_row, w_head_b, examples):
    pooled, logits = head_logits(tok_act, w_head_b)
    soft_prob = jax.nn.softmax(logits, axis=-1)
    onehot = (lab_row[:, None] == jnp.arange(logits.shape[1])[None, :]).astype(jnp.float32)
    d_logits = ((soft_prob - onehot) / examples).astype(jnp.bfloat16)
    g_head = jnp.einsum('bd,bc->dc', pooled, d_logits, preferred_element_type=jnp.float32)
    d_pooled = jnp.einsum('bc,dc->bd', d_logits, w_head_b, preferred_element_type=jnp.float32)
    d_top = jnp.broadcast_to((d_pooled / tok_act.shape[1])[:, None, :], tok_act.shape)
    return g_head, d_top


def next_logits(images, new_w_in, new_w_out, new_w_head):
    w_in_b = new_w_in.astype(jnp.bfloat16)
    w_out_b = new_w_out.astype(jnp.bfloat16)
    tok_act = images
    for layer_idx in range(new_w_in.shape[0]):
        tok_act, _ = block_forward(tok_act, w_in_b[layer_idx], w_out_b[layer_idx])
    return head_logits(tok_act, new_w_head.astype(jnp.bfloat16))[1]


def solution(mesh):
    group_size = mesh.shape['data']

    def local_step(x_step, labels, x_next, w_in, w_out, w_head, mom_in, mom_out, mom_head, learn_rate, mom_coef):
        micro_count = x_step.shape[0]
        layers = w_in.shape[0]
        examples = micro_count * x_step.shape[1] * group_size
        w_in_b = w_in.astype(jnp.bfloat16)
        w_out_b = w_out.astype(jnp.bfloat16)
        w_head_b = w_head.astype(jnp.bfloat16)
        sum_in = [None] * layers
        sum_out = [None] * layers
        red_in = [None] * layers
        red_out = [None] * layers
        sum_head = None
        red_head = None
        for step_index in range(micro_count):
            last_micro = step_index == micro_count - 1
            tok_act = x_step[step_index]
            kept_in = []
            kept_act = []
            for layer_idx in range(layers):
                kept_in.append(tok_act)
                tok_act, saved_act = block_forward(tok_act, w_in_b[layer_idx], w_out_b[layer_idx])
                kept_act.append(saved_act)
            g_head, d_act = head_backward(tok_act, labels[step_index], w_head_b, examples)
            sum_head = g_head if sum_head is None else sum_head + g_head
            if last_micro:
                red_head = lax.psum(sum_head.astype(jnp.bfloat16), 'data')
            for layer_idx in reversed(range(layers)):
                g_one, g_two, d_act = block_backward(kept_in[layer_idx], kept_act[layer_idx], d_act, w_in_b[layer_idx], w_out_b[layer_idx], layer_idx > 0)
                sum_out[layer_idx] = g_two if sum_out[layer_idx] is None else sum_out[layer_idx] + g_two
                sum_in[layer_idx] = g_one if sum_in[layer_idx] is None else sum_in[layer_idx] + g_one
                if last_micro:
                    red_out[layer_idx] = lax.psum(sum_out[layer_idx].astype(jnp.bfloat16), 'data')
                    red_in[layer_idx] = lax.psum(sum_in[layer_idx].astype(jnp.bfloat16), 'data')
        new_mom_in = mom_coef * mom_in + jnp.stack(red_in).astype(jnp.float32)
        new_mom_out = mom_coef * mom_out + jnp.stack(red_out).astype(jnp.float32)
        new_mom_head = mom_coef * mom_head + red_head.astype(jnp.float32)
        new_w_in = w_in - learn_rate * new_mom_in
        new_w_out = w_out - learn_rate * new_mom_out
        new_w_head = w_head - learn_rate * new_mom_head
        logits_next = next_logits(x_next, new_w_in, new_w_out, new_w_head)
        return (logits_next, new_w_in, new_w_out, new_w_head, new_mom_in, new_mom_out, new_mom_head)

    return jax.shard_map(local_step, mesh=mesh, in_specs=(P(None, 'data', None, None), P(None, 'data'), P('data', None, None), P(), P(), P(), P(), P(), P(), P(), P()), out_specs=(P('data', None), P(), P(), P(), P(), P(), P()), check_vma=False)
```

profile of v0, /device:TPU:0, one launch (start us, length us, event | category | flops | bytes accessed | tf_op | source)
XLA Modules:
  0.0 1485.8 jit_solution(1043601506457490458)
XLA Ops:
  7.2 20.7 %convert_element_type.311 = bf16[4,3072,768]{2,1,0:T(8,128)(2,1)} convert(f32[4,3072,768]{2,1,0:T(8,128)} %param.15) | non-fusion elementwise | flops 9437184 | bytes 56623104 | tf_op jit(solution)/shard_map/convert_element_type | solution.py:73
  63.5 12.3 convert_reduce_fusion.9
  89.8 12.2 convert_reduce_fusion.8
  156.0 13.4 fusion.305
  169.4 16.1 %fusion.27 = bf16[2,576,3072]{2,1,0:T(8,128)(2,1)} fusion(f32[2,576,3072]{2,1,0:T(8,128)} %fusion.234, bf16[4,3072,768]{2,1,0:T(8,128)(2,1)S(1)} %bitcast.308, bf16[2,768]{1,0:T(2,128)(2,1)S(1)} %get-tuple-element.46), kind=kOutput, calls=%fused_computation.51 | convolution fusion | flops 5506596864 | bytes 25955328 | tf_op jit(solution)/shard_map/bsd,fd->bsf/dot_general | solution.py:29
  196.9 18.1 %fusion.310 = f32[3072,768,1]{1,0,2:T(8,128)} fusion(f32[2,576]{1,0:T(2,128)S(1)} %negate_multiply_fusion.5, f32[2,768]{1,0:T(2,128)S(1)} %copy-done.71, bf16[2,576,768]{2,1,0:T(8,128)(2,1)S(1)} %get-tuple-element.35, f32[2,576,768]{2,1,0:T(8,128)S(1)} %get-tuple-element.51, f32[2,576]{1,0:T(2,128)S(1)} %multiply_multiply_fusion.25, ...), kind=kOutput, calls=%fused_computation.379 | convolution fusion | flops 5475631104 | bytes 28925952 | tf_op jit(solution)/shard_map/bsf,bsd->fd/dot_general | solution.py:28
  214.9 18.6 %fusion.20 = bf16[2,576,3072]{2,1,0:T(8,128)(2,1)} fusion(f32[2,576,3072]{2,1,0:T(8,128)} %fusion.228, bf16[4,3072,768]{2,1,0:T(8,128)(2,1)} %convert_element_type.311, f32[2,576]{1,0:T(2,128)S(1)} %negate_multiply_fusion.5, f32[2,768]{1,0:T(2,128)S(1)} %copy-done.71, bf16[2,576,768]{2,1,0:T(8,128)(2,1)S(1)} %get-tuple-element.35, ...), kind=kOutput, calls=%fused_computation.44 | convolution fusion | flops 5514559488 | bytes 31285248 | tf_op jit(solution)/shard_map/bsd,fd->bsf/dot_general | solution.py:29
  247.3 14.9 %fusion.302 = f32[3072,768,1]{1,0,2:T(8,128)} fusion(f32[2,576,768]{2,1,0:T(8,128)S(1)} %add_add_fusion.8, f32[2,576,3072]{2,1,0:T(8,128)} %fusion.222), kind=kOutput, calls=%fused_computation.373 | convolution fusion | flops 5468553216 | bytes 27131904 | tf_op jit(solution)/shard_map/bsf,bsd->fd/dot_general | solution.py:28
  262.2 17.5 %fusion.13 = bf16[2,576,3072]{2,1,0:T(8,128)(2,1)} fusion(f32[2,576,3072]{2,1,0:T(8,128)} %fusion.222, bf16[4,3072,768]{2,1,0:T(8,128)(2,1)} %convert_element_type.311, f32[2,576,768]{2,1,0:T(8,128)S(1)} %add_add_fusion.8), kind=kOutput, calls=%fused_computation.37 | convolution fusion | flops 5507481600 | bytes 29491200 | tf_op jit(solution)/shard_map/bsd,fd->bsf/dot_general | solution.py:29
  279.7 12.1 fusion.283
  291.9 12.5 fusion.286
  336.8 12.1 convert_reduce_fusion.5
  387.5 13.1 convert_reduce_fusion.3
  412.8 11.9 convert_reduce_fusion.13
  429.7 15.9 %fusion.55 = bf16[2,576,3072]{2,1,0:T(8,128)(2,1)} fusion(f32[2,576,3072]{2,1,0:T(8,128)} %fusion.232, bf16[4,3072,768]{2,1,0:T(8,128)(2,1)S(1)} %bitcast.312, bf16[2,768]{1,0:T(2,128)(2,1)S(1)} %get-tuple-element.48), kind=kOutput, calls=%fused_computation.79 | convolution fusion | flops 5506596864 | bytes 25955328 | tf_op jit(solution)/shard_map/bsd,fd->bsf/dot_general | solution.py:29
  445.7 14.4 fusion.147
  470.0 18.3 %fusion.48 = bf16[2,576,3072]{2,1,0:T(8,128)(2,1)} fusion(f32[2,576,3072]{2,1,0:T(8,128)} %fusion.226, bf16[4,3072,768]{2,1,0:T(8,128)(2,1)} %convert_element_type.311, f32[2,576]{1,0:T(2,128)S(1)} %negate_multiply_fusion.2, f32[2,768]{1,0:T(2,128)S(1)} %get-tuple-element.49, bf16[2,576,768]{2,1,0:T(8,128)(2,1)S(1)} %get-tuple-element.43, ...), kind=kOutput, calls=%fused_computation.72 | convolution fusion | flops 5514559488 | bytes 31285248 | tf_op jit(solution)/shard_map/bsd,fd->bsf/dot_general | solution.py:29
  488.3 16.6 %fusion.146 = bf16[1,3072,768]{2,1,0:T(8,128)(2,1)} fusion(f32[3072,768,1]{1,0,2:T(8,128)} %fusion.310, f32[2,576]{1,0:T(2,128)S(1)} %negate_multiply_fusion.2, f32[2,768]{1,0:T(2,128)S(1)} %get-tuple-element.49, bf16[2,576,768]{2,1,0:T(8,128)(2,1)S(1)} %get-tuple-element.43, f32[2,576,768]{2,1,0:T(8,128)S(1)} %get-tuple-element.53, ...), kind=kOutput, calls=%fused_computation.234 | convolution fusion | flops 5480349696 | bytes 33644544 | tf_op jit(solution)/shard_map/bsf,bsd->fd/dot_general | solution.py:28
  519.2 17.4 %fusion.41 = bf16[2,576,3072]{2,1,0:T(8,128)(2,1)} fusion(f32[2,576,3072]{2,1,0:T(8,128)} %fusion.220, bf16[4,3072,768]{2,1,0:T(8,128)(2,1)} %convert_element_type.311, f32[2,576,768]{2,1,0:T(8,128)S(1)} %add_add_fusion.6), kind=kOutput, calls=%fused_computation.65 | convolution fusion | flops 5507481600 | bytes 29491200 | tf_op jit(solution)/shard_map/bsd,fd->bsf/dot_general | solution.py:29
  536.6 14.9 %fusion.145 = bf16[1,3072,768]{2,1,0:T(8,128)(2,1)} fusion(f32[3072,768,1]{1,0,2:T(8,128)} %fusion.302, f32[2,576,768]{2,1,0:T(8,128)S(1)} %add_add_fusion.6, f32[2,576,3072]{2,1,0:T(8,128)} %fusion.220), kind=kOutput, calls=%fused_computation.233 | convolution fusion | flops 5473271808 | bytes 31850496 | tf_op jit(solution)/shard_map/bsf,bsd->fd/dot_general | solution.py:28
  579.7 23.0 %fusion.104 = f32[768,3072,1]{1,0,2:T(8,128)} fusion(f32[2,576,3072]{2,1,0:T(8,128)} %fusion.166, bf16[2,576,768]{2,1,0:T(8,128)(2,1)} %add_convert_fusion, bf16[4,3072,768]{2,1,0:T(8,128)(2,1)} %convert_element_type.311, f32[2,576]{1,0:T(2,128)} %copy-done.73, f32[2,576]{1,0:T(2,128)} %copy-done.68, bf16[2,2,576,768]{3,2,1,0:T(8,128)(2,1)} %param.11), kind=kOutput, calls=%fused_computation.140 | convolution fusion | flops 10945953792 | bytes 31860736 | tf_op jit(solution)/shard_map/bsd,bsf->df/dot_general | solution.py:32
  602.7 14.9 fusion.144
  617.6 12.9 fusion.143
  630.5 12.9 fusion.142
  652.3 25.4 %fusion.138 = bf16[1,768,3072]{2,1,0:T(8,128)(2,1)} fusion(f32[768,3072,1]{1,0,2:T(8,128)} %fusion.104, f32[2,576,3072]{2,1,0:T(8,128)} %fusion.167, f32[2,576]{1,0:T(2,128)} %copy-done.72, f32[2,576]{1,0:T(2,128)S(1)} %copy-done.67, bf16[2,576,768]{2,1,0:T(8,128)(2,1)S(1)} %copy-done.29, bf16[4,3072,768]{2,1,0:T(8,128)(2,1)} %convert_element_type.311, ...), kind=kOutput, calls=%fused_computation.228 | convolution fusion | flops 10950672384 | bytes 36578816 | tf_op jit(solution)/shard_map/bsd,bsf->df/dot_general | solution.py:32
  680.2 574.7 %all-reduce.3.cloned.1.call-done = (bf16[768,1000]{0,1:T(8,128)(2,1)}, bf16[1,3072,768]{2,1,0:T(8,128)(2,1)}, bf16[1,3072,768]{2,1,0:T(8,128)(2,1)}, bf16[1,3072...) async-done(((bf16[768,1000]{0,1:T(8,128)(2,1)}, ...) | async-done | bytes 39284752 | tf_op jit(solution)/shard_map/psum | solution.py:93
  1254.9 64.5 %fusion.361 = (bf16[4,768,3072]{2,1,0:T(8,128)(2,1)}, f32[4,768,3072]{2,1,0:T(8,128)}, f32[4,768,3072]{2,1,0:T(8,128)}) fusion(f32[4,768,3072]{2,1,0:T(8,128)} %param.14, f32[]{:T(128)S(6)} %copy.27, bf16[1,768,3072]{2,1,0:T(8,128)(2,1)} %get-tuple-element.16, bf16[1,768,3072]{2,1,0:T(8,128)(2,1)} %get-tuple-element.17, ...), kind=kLoop, calls=%fused_computation.477 | loop fusion | flops 84934656 | bytes 188743680 | tf_op jit(solution)/shard_map/convert_element_type | solution.py:57
  1330.8 59.6 %fusion.362 = (bf16[4,3072,768]{2,1,0:T(8,128)(2,1)}, f32[4,3072,768]{2,1,0:T(8,128)}, f32[4,3072,768]{2,1,0:T(8,128)}) fusion(f32[4,3072,768]{2,1,0:T(8,128)} %param.15, f32[]{:T(128)S(6)} %copy.27, bf16[1,3072,768]{2,1,0:T(8,128)(2,1)S(1)} %copy-done.25, bf16[1,3072,768]{2,1,0:T(8,128)(2,1)S(1)} %copy-done.26, ...), kind=kLoop, calls=%fused_computation.478 | loop fusion | flops 84934656 | bytes 188743680 | tf_op jit(solution)/shard_map/convert_element_type | solution.py:58
  1390.4 12.9 convert_reduce_fusion.2
  1415.5 13.3 convert_reduce_fusion.1
  1438.6 12.9 convert_reduce_fusion
  1461.6 12.9 convert_reduce_fusion.12
  (321 shorter events, 325.6 us)
Async XLA Ops:
  7.2 1247.7 %all-reduce.3.cloned.1.call-start = ((), (), s32[]{:S(2)}) async-start(), calls=%async_computation | async-start | bytes 78569472 | tf_op jit(solution)/shard_map/psum | solution.py:93
  7.2 29.5 %copy-start = (f32[4,768,3072]{2,1,0:T(8,128)S(1)}, f32[4,768,3072]{2,1,0:T(8,128)}, u32[]{:S(2)}) copy-start(f32[4,768,3072]{2,1,0:T(8,128)} %param.14) | copy-start | bytes 113246208
  47.7 15.8 %slice-start = ((s8[18874368]{0:T(1024)(128)(4,1)}), s8[4194304]{0:T(1024)(128)(4,1)S(1)}, s32[]{:S(2)}) async-start(s8[18874368]{0:T(1024)(128)(4,1)} %bitcast.307), calls=%async_computation.1 | async-start | bytes 8388608
  126.9 68.1 %copy-start.49 = (f32[2,576]{1,0:T(2,128)}, f32[2,576]{1,0:T(2,128)S(1)}, u32[]{:S(2)}) copy-start(f32[2,576]{1,0:T(2,128)S(1)} %broadcast_multiply_fusion.7) | copy-start | bytes 13828
  127.7 67.4 %copy-start.64 = (f32[2,576]{1,0:T(2,128)}, f32[2,576]{1,0:T(2,128)S(1)}, u32[]{:S(2)}) copy-start(f32[2,576]{1,0:T(2,128)S(1)} %fusion.318) | copy-start | bytes 13828
  196.8 18.1 %copy-start.50 = (f32[2,576]{1,0:T(2,128)S(1)}, f32[2,576]{1,0:T(2,128)}, u32[]{:S(2)}) copy-start(f32[2,576]{1,0:T(2,128)} %copy-done.49) | copy-start | bytes 13828
  196.9 18.1 %copy-start.65 = (f32[2,576]{1,0:T(2,128)S(1)}, f32[2,576]{1,0:T(2,128)}, u32[]{:S(2)}) copy-start(f32[2,576]{1,0:T(2,128)} %copy-done.64) | copy-start | bytes 13828
  214.9 18.6 %copy-start.10 = (bf16[2,576,768]{2,1,0:T(8,128)(2,1)S(1)}, bf16[2,576,768]{2,1,0:T(8,128)(2,1)}, u32[]{:S(2)}) copy-start(bf16[2,576,768]{2,1,0:T(8,128)(2,1)} %copy-done.9) | copy-start | bytes 5308420
  214.9 18.6 %copy-start.48 = (f32[2,576]{1,0:T(2,128)S(1)}, f32[2,576]{1,0:T(2,128)}, u32[]{:S(2)}) copy-start(f32[2,576]{1,0:T(2,128)} %copy-done.47) | copy-start | bytes 13828
  247.3 14.9 %copy-start.14 = (f32[2,576,768]{2,1,0:T(8,128)}, f32[2,576,768]{2,1,0:T(8,128)S(1)}, u32[]{:S(2)}) copy-start(f32[2,576,768]{2,1,0:T(8,128)S(1)} %add_add_fusion.8) | copy-start | bytes 10616836
  279.7 24.7 %slice-start.25 = ((s8[7077888]{0:T(1024)(128)(4,1)}), s8[2883584]{0:T(1024)(128)(4,1)S(1)}, s32[]{:S(2)}) async-start(s8[7077888]{0:T(1024)(128)(4,1)} %bitcast.319), calls=%async_computation.26 | async-start | bytes 5767168
  315.1 21.6 %slice-start.5 = ((s8[18874368]{0:T(1024)(128)(4,1)}), s8[4194304]{0:T(1024)(128)(4,1)S(1)}, s32[]{:S(2)}) async-start(s8[18874368]{0:T(1024)(128)(4,1)} %bitcast.309), calls=%async_computation.6 | async-start | bytes 8388608
  315.1 21.6 %slice-start.6 = ((s8[18874368]{0:T(1024)(128)(4,1)}), s8[4194304]{0:T(1024)(128)(4,1)S(1)}, s32[]{:S(2)}) async-start(s8[18874368]{0:T(1024)(128)(4,1)} %bitcast.309), calls=%async_computation.7 | async-start | bytes 8388608
  387.5 25.3 %slice-start.10 = ((s8[18874368]{0:T(1024)(128)(4,1)}), s8[2097152]{0:T(1024)(128)(4,1)S(1)}, s32[]{:S(2)}) async-start(s8[18874368]{0:T(1024)(128)(4,1)} %bitcast.311), calls=%async_computation.11 | async-start | bytes 4194304
  387.5 25.3 %slice-start.11 = ((s8[18874368]{0:T(1024)(128)(4,1)}), s8[4194304]{0:T(1024)(128)(4,1)S(1)}, s32[]{:S(2)}) async-start(s8[18874368]{0:T(1024)(128)(4,1)} %bitcast.311), calls=%async_computation.12 | async-start | bytes 8388608
  387.5 25.3 %slice-start.12 = ((s8[18874368]{0:T(1024)(128)(4,1)}), s8[4194304]{0:T(1024)(128)(4,1)S(1)}, s32[]{:S(2)}) async-start(s8[18874368]{0:T(1024)(128)(4,1)} %bitcast.311), calls=%async_computation.13 | async-start | bytes 8388608
  387.5 25.3 %slice-start.13 = ((s8[18874368]{0:T(1024)(128)(4,1)}), s8[4194304]{0:T(1024)(128)(4,1)S(1)}, s32[]{:S(2)}) async-start(s8[18874368]{0:T(1024)(128)(4,1)} %bitcast.311), calls=%async_computation.14 | async-start | bytes 8388608
  401.3 114.6 %copy-start.42 = (f32[2,576]{1,0:T(2,128)}, f32[2,576]{1,0:T(2,128)S(1)}, u32[]{:S(2)}) copy-start(f32[2,576]{1,0:T(2,128)S(1)} %fusion.321) | copy-start | bytes 13828
  468.6 19.7 %copy-start.16 = (f32[2,576,768]{2,1,0:T(8,128)}, f32[2,576,768]{2,1,0:T(8,128)S(1)}, u32[]{:S(2)}) copy-start(f32[2,576,768]{2,1,0:T(8,128)S(1)} %get-tuple-element.53) | copy-start | bytes 10616836
  488.3 16.6 %copy-start.4 = (bf16[2,576,768]{2,1,0:T(8,128)(2,1)S(1)}, bf16[2,576,768]{2,1,0:T(8,128)(2,1)}, u32[]{:S(2)}) copy-start(bf16[2,576,768]{2,1,0:T(8,128)(2,1)} %copy-done.3) | copy-start | bytes 5308420
  488.3 16.6 %copy-start.34 = (f32[2,576]{1,0:T(2,128)S(1)}, f32[2,576]{1,0:T(2,128)}, u32[]{:S(2)}) copy-start(f32[2,576]{1,0:T(2,128)} %copy-done.33) | copy-start | bytes 13828
  536.6 14.9 %copy-start.2 = (bf16[2,576,768]{2,1,0:T(8,128)(2,1)S(1)}, bf16[2,576,768]{2,1,0:T(8,128)(2,1)}, u32[]{:S(2)}) copy-start(bf16[2,576,768]{2,1,0:T(8,128)(2,1)} %copy-done.1) | copy-start | bytes 5308420
  536.6 14.9 %copy-start.32 = (f32[2,576]{1,0:T(2,128)S(1)}, f32[2,576]{1,0:T(2,128)}, u32[]{:S(2)}) copy-start(f32[2,576]{1,0:T(2,128)} %copy-done.31) | copy-start | bytes 13828
  551.5 17.4 %slice-start.27 = ((s8[14155776]{0:T(1024)(128)(4,1)}), s8[4194304]{0:T(1024)(128)(4,1)S(1)}, s32[]{:S(2)}) async-start(s8[14155776]{0:T(1024)(128)(4,1)} %bitcast.321), calls=%async_computation.28 | async-start | bytes 8388608
  551.5 17.4 %slice-start.28 = ((s8[14155776]{0:T(1024)(128)(4,1)}), s8[4194304]{0:T(1024)(128)(4,1)S(1)}, s32[]{:S(2)}) async-start(s8[14155776]{0:T(1024)(128)(4,1)} %bitcast.321), calls=%async_computation.29 | async-start | bytes 8388608
  551.5 17.4 %slice-start.29 = ((s8[14155776]{0:T(1024)(128)(4,1)}), s8[4194304]{0:T(1024)(128)(4,1)S(1)}, s32[]{:S(2)}) async-start(s8[14155776]{0:T(1024)(128)(4,1)} %bitcast.321), calls=%async_computation.30 | async-start | bytes 8388608
  602.7 14.9 %copy-start.43 = (f32[2,576]{1,0:T(2,128)S(1)}, f32[2,576]{1,0:T(2,128)}, u32[]{:S(2)}) copy-start(f32[2,576]{1,0:T(2,128)} %copy-done.42) | copy-start | bytes 13828
  617.6 25.8 %slice-start.20 = ((s8[9437184]{0:T(1024)(128)(4,1)}), s8[4194304]{0:T(1024)(128)(4,1)S(1)}, s32[]{:S(2)}) async-start(s8[9437184]{0:T(1024)(128)(4,1)} %bitcast.315), calls=%async_computation.21 | async-start | bytes 8388608
  617.6 25.8 %slice-start.21 = ((s8[9437184]{0:T(1024)(128)(4,1)}), s8[4194304]{0:T(1024)(128)(4,1)S(1)}, s32[]{:S(2)}) async-start(s8[9437184]{0:T(1024)(128)(4,1)} %bitcast.315), calls=%async_computation.22 | async-start | bytes 8388608
  617.6 25.8 %slice-start.23 = ((s8[7077888]{0:T(1024)(128)(4,1)}), s8[4194304]{0:T(1024)(128)(4,1)S(1)}, s32[]{:S(2)}) async-start(s8[7077888]{0:T(1024)(128)(4,1)} %bitcast.317), calls=%async_computation.24 | async-start | bytes 8388608
  1404.0 25.5 %slice-start.15 = ((s8[18874368]{0:T(1024)(128)(4,1)}), s8[4194304]{0:T(1024)(128)(4,1)S(1)}, s32[]{:S(2)}) async-start(s8[18874368]{0:T(1024)(128)(4,1)} %bitcast.313), calls=%async_computation.16 | async-start | bytes 8388608
  1404.0 25.5 %slice-start.16 = ((s8[18874368]{0:T(1024)(128)(4,1)}), s8[4194304]{0:T(1024)(128)(4,1)S(1)}, s32[]{:S(2)}) async-start(s8[18874368]{0:T(1024)(128)(4,1)} %bitcast.313), calls=%async_computation.17 | async-start | bytes 8388608
  (77 other events, 621.8 us)
Sparse Core Ops, SparseCore 0:
  677.8 576.9 all-reduce.2
where the time goes:
time: 1490 us
  matrix products  688 us (46%)
  waiting for transfers between devices  575 us (39%)
  other arithmetic  188 us (13%)
  local copies, waits for them, and re-layouts  17.6 us (1%)
  between operations  17.3 us (1%)
    psum x1, waiting for transfers between devices, local_step(): red_head = lax.psum(sum_head.astype(jnp.bfloat16), 'data')  575 us
    dot_general x12, matrix products, block_forward(): jnp.einsum('bsf,fd->bsd', hidden, w_two, preferred_element_type=jnp.float32)  149 us
    dot_general x12, matrix products, block_forward(): jnp.einsum('bsd,df->bsf', normed, w_one, preferred_element_type=jnp.float32)  133 us
    dot_general x8, matrix products, block_backward(): jnp.einsum('bsf,bsd->fd', hidden, d_out_b, preferred_element_type=jnp.flo...  118 us
    dot_general x8, matrix products, block_backward(): jnp.einsum('bsd,bsf->df', normed, d_pre, preferred_element_type=jnp.float32)  117 us
    dot_general x6, matrix products, block_backward(): jnp.einsum('bsd,fd->bsf', d_out_b, w_two, preferred_element_type=jnp.floa...  104 us
    convert_element_type x1, other arithmetic, next_logits(): w_in_b = new_w_in.astype(jnp.bfloat16)  64.5 us
    convert_element_type x1, other arithmetic, next_logits(): w_out_b = new_w_out.astype(jnp.bfloat16)  59.6 us
  transfers between devices with their start and end apart: 1, of which 1 were waited for; matrix products, arithmetic and copies ran while one was open for 0% of the time, Pallas kernels for 0%

commit v1 on v0

v1 whole, which is shorter than its diff:
```python
import functools
import math

import jax
import jax.numpy as jnp
from jax import lax
from jax.experimental import pallas as pl
from jax.experimental.pallas import tpu as pltpu
from jax.sharding import PartitionSpec as P

BF16 = jnp.bfloat16
F32 = jnp.float32
LN_EPS = 1e-6
C0 = math.sqrt(2.0 / math.pi)
C1 = 0.044715
CHUNK = 512
ROWS = 256
LANES = 256
FWD_TILE = 768
ACT_ROWS = 64
LN_ROWS = 96
MESH = pl.DeviceIdType.MESH
VMEM_LIMIT = 63 * 1024 * 1024


def norm_stats(x_f32):
    row_mean = jnp.mean(x_f32, axis=-1, keepdims=True)
    centered = x_f32 - row_mean
    inv_std = lax.rsqrt(jnp.mean(centered * centered, axis=-1, keepdims=True) + LN_EPS)
    return centered, inv_std


def norm_rows(x_f32):
    centered, inv_std = norm_stats(x_f32)
    return centered * inv_std


def gelu_parts(pre):
    squared = pre * pre
    gate = 0.5 + 0.5 * jnp.tanh(pre * (C0 + (C0 * C1) * squared))
    return squared, gate, pre * gate


def span(index, size):
    return slice(index * size, index * size + size)


def row_loop(total, step, body):
    @pl.loop(0, total // step)
    def _(index):
        body(pl.ds(pl.multiple_of(index * step, step), step))


def dot(a, b):
    return jnp.dot(a, b, preferred_element_type=F32)


def dot_rhs_t(a, b):
    return lax.dot_general(a, b, (((1,), (1,)), ((), ())), preferred_element_type=F32)


def dot_lhs_t(a, b):
    return lax.dot_general(a, b, (((0,), (0,)), ((), ())), preferred_element_type=F32)


def image_sums(x, image):
    rows = lax.broadcasted_iota(jnp.int32, (8, x.shape[0]), 0)
    cols = lax.broadcasted_iota(jnp.int32, (8, x.shape[0]), 1)
    inside = (cols >= rows * image) & (cols < (rows + 1) * image)
    return dot(inside.astype(F32).astype(BF16), x)


def forward_kernel(
    x_hbm, w_in, w_out, hid, slope, w_in_b, w_out_b, x_out, hid_sum, top_sum,
    x, n, acc, pre, sem, *, tokens, image, tile, layers, chunks,
):
    layer, chunk = pl.program_id(0), pl.program_id(1)

    @pl.when((layer == 0) & (chunk == 0))
    def _():
        load = pltpu.make_async_copy(x_hbm, x, sem)
        load.start()
        load.wait()

    w_in_b[...] = w_in[...].astype(BF16)
    w_out_b[...] = w_out[...].astype(BF16)

    def first(i):
        pre[i % 2] = dot(n[span(i, tile), :], w_in_b[...])

    def act(i):
        for j in range(tile // ACT_ROWS):
            rows = span(i * tile // ACT_ROWS + j, ACT_ROWS)
            squared, gate, value = gelu_parts(pre[i % 2, span(j, ACT_ROWS), :])
            hid[rows, :] = value.astype(BF16)
            slope[rows, :] = (gate + (value * (2 * C0 + (6 * C0 * C1) * squared)) * (1.0 - gate)).astype(BF16)

    def second(i, begin):
        rows = span(i, tile)
        part = dot(hid[rows, :], w_out_b[...])
        acc[rows, :] = part if begin else part + acc[rows, :]

    def begin_rows(i):
        for j in range(tile // LN_ROWS):
            rows = span(i * tile // LN_ROWS + j, LN_ROWS)
            n[rows, :] = norm_rows(x[rows, :].astype(F32)).astype(BF16)

    def end_rows(i):
        for j in range(tile // LN_ROWS):
            rows = span(i * tile // LN_ROWS + j, LN_ROWS)
            value = (x[rows, :].astype(F32) + acc[rows, :]).astype(BF16)
            x[rows, :] = value
            x_out[rows, :] = value

    def run(begin, end):
        steps = [begin_rows] * begin + [first, act, functools.partial(second, begin=begin)] + [end_rows] * end
        count = tokens // tile
        for i in range(count + len(steps) - 1):
            for lag, step in enumerate(steps):
                if 0 <= i - lag < count:
                    step(i - lag)

    @pl.when(chunk == 0)
    def _():
        run(True, False)

    @pl.when((chunk > 0) & (chunk < chunks - 1))
    def _():
        run(False, False)

    @pl.when(chunk == chunks - 1)
    def _():
        run(False, True)

    @pl.when(layer == layers - 1)
    def _():
        hid_sum[...] = image_sums(hid[...], image)

        @pl.when(chunk == chunks - 1)
        def _():
            top_sum[...] = image_sums(x[...], image)


def forward(x, w_in, w_out, image=576):
    tokens, dim = x.shape
    layers, _, hidden = w_in.shape
    chunks = hidden // CHUNK
    top = layers - 1
    one = pl.squeezed
    in_spec = pl.BlockSpec((one, dim, CHUNK), lambda l, f: (l, 0, f))
    out_spec = pl.BlockSpec((one, CHUNK, dim), lambda l, f: (l, f, 0))
    act = jax.ShapeDtypeStruct((layers, chunks, tokens, CHUNK), BF16)
    return pl.pallas_call(
        functools.partial(forward_kernel, tokens=tokens, image=image, tile=FWD_TILE, layers=layers, chunks=chunks),
        grid=(layers, chunks),
        in_specs=[pl.BlockSpec(memory_space=pl.ANY), in_spec, out_spec],
        out_specs=[
            pl.BlockSpec((one, one, tokens, CHUNK), lambda l, f: (l, jnp.where(l == top, 0, f), 0, 0)),
            pl.BlockSpec((one, one, tokens, CHUNK), lambda l, f: (l, f, 0, 0)),
            in_spec,
            out_spec,
            pl.BlockSpec((one, tokens, dim), lambda l, f: (l, 0, 0)),
            pl.BlockSpec((one, 8, CHUNK), lambda l, f: (jnp.where(l == top, f, 0), 0, 0)),
            pl.BlockSpec((8, dim), lambda l, f: (0, 0)),
        ],
        out_shape=[
            act,
            act,
            jax.ShapeDtypeStruct(w_in.shape, BF16),
            jax.ShapeDtypeStruct(w_out.shape, BF16),
            jax.ShapeDtypeStruct((layers, tokens, dim), BF16),
            jax.ShapeDtypeStruct((chunks, 8, CHUNK), F32),
            jax.ShapeDtypeStruct((8, dim), F32),
        ],
        scratch_shapes=[
            pltpu.VMEM((tokens, dim), BF16),
            pltpu.VMEM((tokens, dim), BF16),
            pltpu.VMEM((tokens, dim), F32),
            pltpu.VMEM((2, FWD_TILE, CHUNK), F32),
            pltpu.SemaphoreType.DMA,
        ],
        compiler_params=pltpu.CompilerParams(vmem_limit_bytes=VMEM_LIMIT),
        name="forward",
    )(x, w_in, w_out)


PAIRS = 7
STREAM = 4608
HALF = 2304
COLOR = 1152
SIZES = (576, 288, 144)
MASKS = ((2, 8, 4, 16), (4, 8, 2, 16))
READY = (4, 5)
REDUCE = (0, 1, 3, 5, 6, 7, 8)
GATHER = (8, 9, 10, 12, 14, 15)
TICKS = 24
LAST_TICK = READY[1] + 3 * (PAIRS - 1) + GATHER[-1] + 1
GROUPS = 22
EXTRA_TICKS = {5: 2, 6: 5, 7: 8, 8: 11, 9: 15, 10: 19}


def add_into(dst, src, rows):
    step = min(rows, 288)

    def body(part):
        dst[part, :] = dst[part, :] + src[part, :]

    if rows == step:
        dst[...] = dst[...] + src[...]
    else:
        row_loop(rows, step, body)


def backward_kernel(
    hid, slope, x_in, x_mid, w_in_b, w_out_b, d_top, d_hid_top, extra, total, images_all,
    unit, r0, r1, r2, r3, r4, b_slope, b_hid, b_in, b_out, d_pre, d_x, n, x_buf, d_n,
    load_sem, x_sem, send_sem, recv_sem, local_sem, extra_send, extra_recv, extra_local, *, tokens, image, chunks,
):
    me = lax.axis_index("data")
    core, x_bit, y_bit = me % 2, (me // 2) % 2, (me // 4) % 2
    z_low, z_high = (me // 8) % 2, me // 16
    bits = ((x_bit, z_low, y_bit, z_high), (y_bit, z_low, x_bit, z_high))
    flips = {1: core, 2: x_bit, 4: y_bit, 8: z_low, 16: z_high}

    def peer(mask):
        return (me + mask * (1 - 2 * flips[mask]),)

    def rows_at(start, size):
        return pl.ds(pl.multiple_of(start, 16), size)

    def remote(src, dst, send, recv, mask):
        return pltpu.make_async_remote_copy(
            src_ref=src, dst_ref=dst, send_sem=send, recv_sem=recv, device_id=peer(mask), device_id_type=MESH
        )

    def base(stream, color, level):
        start = stream * STREAM + core * HALF + color * COLOR
        for step in range(level):
            start = start + bits[color][step] * SIZES[step]
        return start

    def lanes_at(bit):
        return pl.ds(pl.multiple_of(bit * 128, 128), 128)

    def piece_of(stream, color, pair):
        return total.at[pair, rows_at(base(stream, color, 3), SIZES[2]), lanes_at(z_high)]

    def copy_of(stage, stream, color, pair, slot):
        bit = bits[color]
        if stage == 0:
            src = unit.at[slot, rows_at(stream * STREAM + (1 - core) * HALF, HALF)]
            dst, mask = r0.at[slot, stream], 1
        elif stage == 1:
            src = r0.at[slot, stream, rows_at(color * COLOR + (1 - bit[0]) * SIZES[0], SIZES[0])]
            dst, mask = r1.at[pair % 3, stream, color], MASKS[color][0]
        elif stage <= 3:
            size = SIZES[stage - 1]
            src = (r1, r2)[stage - 2].at[(pair % 3, slot)[stage - 2], stream, color, rows_at((1 - bit[stage - 1]) * size, size)]
            dst, mask = (r2, r3)[stage - 2].at[slot, stream, color], MASKS[color][stage - 1]
        elif stage == 4:
            src = r3.at[slot, stream, color, :, lanes_at(1 - z_high)]
            dst, mask = r4.at[slot, stream, color], 16
        elif stage == 5:
            src = dst = piece_of(stream, color, pair)
            mask = 16
        elif stage <= 8:
            level = 9 - stage
            src = dst = total.at[pair, rows_at(base(stream, color, level), SIZES[level - 1])]
            mask = MASKS[color][level - 1]
        else:
            src = dst = total.at[pair, rows_at(base(stream, color, 0), COLOR)]
            mask = 1
        at = (stage, color, slot, stream)
        return remote(src, dst, send_sem.at[at], recv_sem.at[at], mask)

    def own_copy(stream, color, pair, slot):
        return pltpu.make_async_copy(
            r4.at[slot, stream, color], piece_of(stream, color, pair), local_sem.at[color, slot, stream]
        )

    def reduce_stage(stage, stream, pair):
        slot = pair % 2
        if stage == 0:
            copy_of(0, stream, 0, pair, slot).start()
            return
        if stage == 1:
            copy_of(0, stream, 0, pair, slot).wait()
            add_into(r0.at[slot, stream], unit.at[slot, rows_at(stream * STREAM + core * HALF, HALF)], HALF)
        for color in range(2):
            bit = bits[color]
            if 2 <= stage <= 5:
                copy_of(stage - 1, stream, color, pair, slot).wait()
            if stage == 2:
                kept = r0.at[slot, stream, rows_at(color * COLOR + bit[0] * SIZES[0], SIZES[0])]
                add_into(r1.at[pair % 3, stream, color], kept, SIZES[0])
            elif stage in (3, 4):
                size = SIZES[stage - 2]
                kept = (r1, r2)[stage - 3].at[(pair % 3, slot)[stage - 3], stream, color, rows_at(bit[stage - 2] * size, size)]
                add_into((r2, r3)[stage - 3].at[slot, stream, color], kept, size)
            elif stage == 5:
                kept = r3.at[slot, stream, color, :, lanes_at(z_high)]
                add_into(r4.at[slot, stream, color], kept, SIZES[2])
        for color in range(2):
            if stage <= 4:
                copy_of(stage, stream, color, pair, slot).start()
            elif stage == 5:
                own_copy(stream, color, pair, slot).start()
            else:
                own_copy(stream, color, pair, slot).wait()

    def gather_step(step, stream, pair):
        slot = pair % 2
        for color in range(2):
            if step > 0:
                copy_of(4 + step, stream, color, pair, slot).wait()
            if step < len(GATHER) - 1:
                copy_of(5 + step, stream, color, pair, slot).start()

    def exchange(tick, first=False):
        def at(offset, stream, action):
            ahead = tick - READY[stream] - offset

            @pl.when((ahead >= 0) & (ahead < 3 * PAIRS) & (ahead % 3 == 0))
            def _():
                action(ahead // 3)

        for stage in reversed(range(2 if first else len(REDUCE))):
            for stream in range(2):
                at(REDUCE[stage], stream, functools.partial(reduce_stage, stage, stream))
        for step in reversed(range(0 if first else len(GATHER))):
            for stream in range(2):
                at(GATHER[step], stream, functools.partial(gather_step, step, stream))

    def extra_rows(level):
        start, size = core * 16, 16
        for step in range(level):
            size = size // 2
            start = start + bits[0][step] * size
        return images_all.at[:, pl.ds(pl.multiple_of(start * 8, 8), size * 8)]

    def extra_copy(stage):
        spot = extra_rows(9 - stage)
        mask = 1 if stage == 9 else MASKS[0][8 - stage]
        src = extra if stage == 5 else spot
        return remote(src, spot, extra_send.at[stage - 5], extra_recv.at[stage - 5], mask)

    def exchange_extra(stage):
        if stage > 5:
            extra_copy(stage - 1).wait()
        if stage == 6:
            pltpu.make_async_copy(extra, extra_rows(4), extra_local).wait()
        if stage == 5:
            pltpu.make_async_copy(extra, extra_rows(4), extra_local).start()
        if stage <= 9:
            extra_copy(stage).start()

    def run_extra(tick, ticks):
        for stage, when in EXTRA_TICKS.items():
            if when in ticks:
                @pl.when(tick == when)
                def _():
                    exchange_extra(stage)

    def load_chunk(tick, top=False):
        layer, chunk, slot = 3 - tick // chunks, tick % chunks, tick % 2
        cols = pl.ds(pl.multiple_of(chunk * CHUNK, CHUNK), CHUNK)
        arrays = [(slope.at[layer, chunk], b_slope), (w_in_b.at[layer, :, cols], b_in)]
        if not top:
            arrays += [(hid.at[layer, chunk], b_hid), (w_out_b.at[layer, cols, :], b_out)]
        return [pltpu.make_async_copy(src, dst.at[slot], load_sem.at[slot, i]) for i, (src, dst) in enumerate(arrays)]

    def load_x(layer):
        return pltpu.make_async_copy(x_mid.at[layer - 1], x_buf.at[layer % 2], x_sem.at[layer % 2])

    load_bottom = pltpu.make_async_copy(x_in, x_buf.at[0], x_sem.at[0])

    for load in load_chunk(0, True):
        load.start()
    load_x(3).start()
    load_x(2).start()

    barrier = pltpu.get_barrier_semaphore()
    for mask in flips:
        pl.semaphore_signal(barrier, inc=1, device_id=peer(mask), device_id_type=MESH)

    def store_in(slot, block, value):
        value = value.astype(BF16)
        for half in range(CHUNK // LANES):
            rows = pl.ds(pl.multiple_of(block * 1536 + half * 768, 16), 768)
            unit[slot, rows, :] = value[:, span(half, LANES)]

    def store_out(slot, block, value):
        value = value.astype(BF16)
        for third in range(768 // LANES):
            rows = pl.ds(pl.multiple_of(block * 1536 + third * CHUNK, 16), CHUNK)
            unit[slot, rows, :] = value[:, span(third, LANES)]

    tile = 768

    def add_d_n(slot):
        for i in range(tokens // tile):
            rows = span(i, tile)
            d_n[rows, :] = dot_rhs_t(d_pre[rows, :], b_in[slot]) + d_n[rows, :]

    load_x(3).wait()

    def start_top(rows):
        n[rows, :] = norm_rows(x_buf[1, rows, :].astype(F32)).astype(BF16)
        d_n[rows, :] = jnp.zeros_like(d_n[rows, :])

    row_loop(tokens, ROWS, start_top)
    for i in range(tokens // image):
        d_x[span(i, image), :] = jnp.broadcast_to(d_top[span(i, 1), :], (image, d_top.shape[1])).astype(BF16)

    pl.semaphore_wait(barrier, len(flips))

    @pl.loop(0, chunks)
    def _(tick):
        slot = tick % 2
        for load in load_chunk(tick, True):
            load.wait()

        @pl.when(tick < chunks - 1)
        def _():
            for load in load_chunk(tick + 1, True):
                load.start()

        @pl.when(tick == chunks - 1)
        def _():
            for load in load_chunk(tick + 1):
                load.start()

        for i in range(tokens // image):
            rows = span(i, image)
            d_pre[rows, :] = (b_slope[slot, rows, :].astype(F32) * d_hid_top[tick, span(i, 1), :]).astype(BF16)
        store_in(0, tick, dot_lhs_t(n[...], d_pre[...]))
        add_d_n(slot)
        exchange(tick, True)
        run_extra(tick, range(chunks))

    @pl.loop(chunks, TICKS)
    def _(tick):
        layer, chunk, slot = 3 - tick // chunks, tick % chunks, tick % 2
        use = (tick // 3 - 1) % 2

        @pl.when(chunk == 0)
        def _():
            upper, lower = (layer + 1) % 2, layer % 2
            pltpu.make_async_copy(x_in, x_buf.at[lower], x_sem.at[lower]).wait()

            def step(rows):
                centered, inv_std = norm_stats(x_buf[upper, rows, :].astype(F32))
                x_hat = centered * inv_std
                grad = d_n[rows, :]
                mean_g = jnp.mean(grad, axis=-1, keepdims=True)
                mean_gx = jnp.mean(grad * x_hat, axis=-1, keepdims=True)
                d_x[rows, :] = (d_x[rows, :].astype(F32) + inv_std * (grad - mean_g - x_hat * mean_gx)).astype(BF16)
                n[rows, :] = norm_rows(x_buf[lower, rows, :].astype(F32)).astype(BF16)
                d_n[rows, :] = jnp.zeros_like(d_n[rows, :])

            row_loop(tokens, ROWS, step)

            @pl.when(layer == 2)
            def _():
                load_x(1).start()

            @pl.when(layer == 1)
            def _():
                load_bottom.start()

        for load in load_chunk(tick):
            load.wait()

        @pl.when(tick < TICKS - 1)
        def _():
            for load in load_chunk(tick + 1):
                load.start()

        for i in range(tokens // tile):
            rows = span(i, tile)
            d_pre[rows, :] = (dot_rhs_t(d_x[rows, :], b_out[slot]) * b_slope[slot, rows, :].astype(F32)).astype(BF16)
        store_out(use, 2 * (chunk % 3) + 1, dot_lhs_t(b_hid[slot], d_x[...]))
        store_in(use, 2 * (chunk % 3), dot_lhs_t(n[...], d_pre[...]))

        @pl.when(layer > 0)
        def _():
            add_d_n(slot)

        exchange(tick)
        run_extra(tick, range(chunks, TICKS))

    @pl.loop(TICKS, LAST_TICK)
    def _(tick):
        exchange(tick)


def backward(hid, slope, x_in, x_mid, w_in_b, w_out_b, d_top, d_hid_top, extra, image):
    layers, chunks, tokens, _ = hid.shape
    dim = x_in.shape[1]
    hbm = pl.BlockSpec(memory_space=pl.ANY)
    vmem = pl.BlockSpec(memory_space=pltpu.VMEM)
    act = pltpu.VMEM((tokens, dim), BF16)
    dma = pltpu.SemaphoreType.DMA
    return pl.pallas_call(
        functools.partial(backward_kernel, tokens=tokens, image=image, chunks=chunks),
        in_specs=[hbm] * 6 + [vmem] * 3,
        out_specs=[hbm, hbm],
        out_shape=[
            jax.ShapeDtypeStruct((PAIRS, 2 * STREAM, LANES), BF16),
            jax.ShapeDtypeStruct((GROUPS, 256, LANES), BF16),
        ],
        scratch_shapes=[
            pltpu.VMEM((2, 2 * STREAM, LANES), BF16),
            pltpu.VMEM((2, 2, HALF, LANES), BF16),
            *[pltpu.VMEM((slots, 2, 2, size, LANES), BF16) for slots, size in zip((3, 2, 2), SIZES)],
            pltpu.VMEM((2, 2, 2, SIZES[2], 128), BF16),
            pltpu.VMEM((2, tokens, CHUNK), BF16),
            pltpu.VMEM((2, tokens, CHUNK), BF16),
            pltpu.VMEM((2, dim, CHUNK), BF16),
            pltpu.VMEM((2, CHUNK, dim), BF16),
            pltpu.VMEM((tokens, CHUNK), BF16),
            act,
            act,
            pltpu.VMEM((2, tokens, dim), BF16),
            pltpu.VMEM((tokens, dim), F32),
            dma((2, 4)),
            dma((2,)),
            dma((10, 2, 2, 2)),
            dma((10, 2, 2, 2)),
            dma((2, 2, 2)),
            dma((5,)),
            dma((5,)),
            dma,
        ],
        compiler_params=pltpu.CompilerParams(vmem_limit_bytes=VMEM_LIMIT, collective_id=0, has_side_effects=True),
        name="backward",
    )(hid, slope, x_in, x_mid, w_in_b, w_out_b, d_top, d_hid_top, extra)


SLOTS = 3


def update_kernel(
    rates, x_hbm, w_in, m_in, w_out, m_out, grads, images_all, w_head, m_head,
    new_w_in, new_m_in, new_w_out, new_m_out, new_w_head, new_m_head, next_logits,
    b_w_in, b_m_in, b_w_out, b_m_out, b_g_in, b_g_out, rows_all, x, n, acc, pre, hid, w_in_b, w_out_b,
    load_sem, store_sem, x_sem, rows_sem, *, tokens, image, tile, chunks, layers,
):
    rate, coef = rates[0], rates[1]
    steps = layers * chunks

    def place(step):
        layer, chunk = step // chunks, step % chunks
        cols = pl.ds(pl.multiple_of(chunk * CHUNK, CHUNK), CHUNK)
        return layer, chunk, cols, step % SLOTS

    def loads(step):
        layer, chunk, cols, slot = place(step)
        top = layer // (layers - 1)
        lower = (1 + 2 * (layers - 2 - layer) + chunk // 3) * 6 + 2 * (chunk % 3)
        block = top * chunk + (1 - top) * lower
        arrays = (
            (w_in.at[layer, :, cols], b_w_in),
            (m_in.at[layer, :, cols], b_m_in),
            (w_out.at[layer, cols, :], b_w_out),
            (m_out.at[layer, cols, :], b_m_out),
            (grads.at[block], b_g_in),
            (grads.at[block + 1 - top], b_g_out),
        )
        return [pltpu.make_async_copy(src, dst.at[slot], load_sem.at[slot, i]) for i, (src, dst) in enumerate(arrays)]

    def stores(step):
        layer, chunk, cols, slot = place(step)
        arrays = (
            (b_w_in, new_w_in.at[layer, :, cols]),
            (b_m_in, new_m_in.at[layer, :, cols]),
            (b_w_out, new_w_out.at[layer, cols, :]),
            (b_m_out, new_m_out.at[layer, cols, :]),
        )
        return [pltpu.make_async_copy(src.at[slot], dst, store_sem.at[slot, i]) for i, (src, dst) in enumerate(arrays)]

    load_x = pltpu.make_async_copy(x_hbm, x, x_sem)
    load_rows = pltpu.make_async_copy(images_all, rows_all, rows_sem)
    load_x.start()
    for ahead in range(SLOTS - 1):
        for load in loads(ahead):
            load.start()
    load_rows.start()
    load_x.wait()

    def start(rows):
        n[rows, :] = norm_rows(x[rows, :].astype(F32)).astype(BF16)
        acc[rows, :] = jnp.zeros_like(acc[rows, :])

    row_loop(tokens, 128, start)

    load_rows.wait()
    classes = w_head.shape[0]
    for group in range(0, classes, LANES):
        size = min(LANES, classes - group)
        for part in range(3):
            at = (slice(group, group + size), span(part, LANES))
            grad = dot_lhs_t(rows_all[18 + group // LANES], rows_all[15 + part])[:size]
            moment = coef * m_head[at] + grad
            new_m_head[at] = moment
            new_w_head[at] = w_head[at] - rate * moment

    @pl.loop(0, steps)
    def _(step):
        layer, chunk, _, slot = place(step)
        for load in loads(step):
            load.wait()

        for half in range(CHUNK // LANES):
            cols = span(half, LANES)
            moment = coef * b_m_in[slot, :, cols] + b_g_in[slot, span(half, b_w_in.shape[1]), :].astype(F32)
            weight = b_w_in[slot, :, cols] - rate * moment
            b_m_in[slot, :, cols] = moment
            b_w_in[slot, :, cols] = weight
            w_in_b[:, cols] = weight.astype(BF16)

        def update_out(grad_of):
            for third in range(768 // LANES):
                cols = span(third, LANES)
                moment = coef * b_m_out[slot, :, cols] + grad_of(third)
                weight = b_w_out[slot, :, cols] - rate * moment
                b_m_out[slot, :, cols] = moment
                b_w_out[slot, :, cols] = weight
                w_out_b[:, cols] = weight.astype(BF16)

        @pl.when(layer < layers - 1)
        def _():
            update_out(lambda third: b_g_out[slot, span(third, CHUNK), :].astype(F32))

        @pl.when(layer == layers - 1)
        def _():
            def top_grad(third):
                parts = [dot_lhs_t(rows_all[2 * chunk + half], rows_all[12 + third]) for half in range(2)]
                return jnp.concatenate(parts, axis=0)

            update_out(top_grad)

        for store in stores(step):
            store.start()

        @pl.when(step >= 1)
        def _():
            for store in stores(step - 1):
                store.wait()

        @pl.when(step + SLOTS - 1 < steps)
        def _():
            for load in loads(step + SLOTS - 1):
                load.start()

        def first(i):
            pre[i % 2] = dot(n[span(i, tile), :], w_in_b[...])

        def act(i):
            for j in range(tile // ACT_ROWS):
                rows = span(j, ACT_ROWS)
                hid[i % 2, rows, :] = gelu_parts(pre[i % 2, rows, :])[-1].astype(BF16)

        def second(i):
            rows = span(i, tile)
            acc[rows, :] = dot(hid[i % 2], w_out_b[...]) + acc[rows, :]

        count = tokens // tile
        for i in range(count + 2):
            if i < count:
                first(i)
            if 0 <= i - 1 < count:
                act(i - 1)
            if i >= 2:
                second(i - 2)

        @pl.when(chunk == chunks - 1)
        def _():
            def finish(rows):
                value = (x[rows, :].astype(F32) + acc[rows, :]).astype(BF16)
                x[rows, :] = value
                n[rows, :] = norm_rows(value.astype(F32)).astype(BF16)
                acc[rows, :] = jnp.zeros_like(acc[rows, :])

            row_loop(tokens, 128, finish)

    pooled = (image_sums(x[...], image) / image).astype(BF16)
    next_logits[...] = dot_rhs_t(pooled, new_w_head[...].astype(BF16))
    for store in stores(steps - 1):
        store.wait()


def update_and_next(rates, x, w_in, m_in, w_out, m_out, total, images_all, w_head, m_head, image=576):
    tokens, dim = x.shape
    layers, _, hidden = w_in.shape
    chunks = hidden // CHUNK
    tile = 384
    hbm = pl.BlockSpec(memory_space=pl.ANY)
    vmem = pl.BlockSpec(memory_space=pltpu.VMEM)
    dma = pltpu.SemaphoreType.DMA
    return pl.pallas_call(
        functools.partial(update_kernel, tokens=tokens, image=image, tile=tile, chunks=chunks, layers=layers),
        in_specs=[pl.BlockSpec(memory_space=pltpu.SMEM)] + [hbm] * 7 + [vmem] * 2,
        out_specs=[hbm] * 4 + [vmem] * 3,
        out_shape=[
            jax.ShapeDtypeStruct(w_in.shape, F32),
            jax.ShapeDtypeStruct(w_in.shape, F32),
            jax.ShapeDtypeStruct(w_out.shape, F32),
            jax.ShapeDtypeStruct(w_out.shape, F32),
            jax.ShapeDtypeStruct(w_head.shape, F32),
            jax.ShapeDtypeStruct(w_head.shape, F32),
            jax.ShapeDtypeStruct((8, w_head.shape[0]), F32),
        ],
        scratch_shapes=[
            pltpu.VMEM((SLOTS, dim, CHUNK), F32),
            pltpu.VMEM((SLOTS, dim, CHUNK), F32),
            pltpu.VMEM((SLOTS, CHUNK, dim), F32),
            pltpu.VMEM((SLOTS, CHUNK, dim), F32),
            pltpu.VMEM((SLOTS, 1536, LANES), BF16),
            pltpu.VMEM((SLOTS, 1536, LANES), BF16),
            pltpu.VMEM((GROUPS, 256, LANES), BF16),
            pltpu.VMEM((tokens, dim), BF16),
            pltpu.VMEM((tokens, dim), BF16),
            pltpu.VMEM((tokens, dim), F32),
            pltpu.VMEM((2, tile, CHUNK), F32),
            pltpu.VMEM((2, tile, CHUNK), BF16),
            pltpu.VMEM((dim, CHUNK), BF16),
            pltpu.VMEM((CHUNK, dim), BF16),
            dma((SLOTS, 6)),
            dma((SLOTS, 4)),
            dma,
            dma,
        ],
        compiler_params=pltpu.CompilerParams(vmem_limit_bytes=VMEM_LIMIT),
        name="update_next",
    )(rates, x, w_in, m_in, w_out, m_out, total.reshape(PAIRS * 6, 1536, LANES), images_all, w_head, m_head)


def solution(mesh):
    group_size = mesh.shape["data"]

    def local_step(x_step, labels, x_next, w_in, w_out, w_head, mom_in, mom_out, mom_head, learn_rate, mom_coef):
        micro, per_micro, image, dim = x_step.shape
        images = micro * per_micro
        layers, _, hidden = w_in.shape
        classes = w_head.shape[1]
        chunks = hidden // CHUNK
        examples = images * group_size
        w_head_b = w_head.astype(BF16)

        x_in = x_step.reshape(images * image, dim)
        hid, slope, w_in_b, w_out_b, x_mid, hid_sum, top_sum = forward(x_in, w_in, w_out, image)

        pooled = (top_sum[:images] / image).astype(BF16)
        soft_prob = jax.nn.softmax(dot(pooled, w_head_b), axis=-1)
        onehot = (labels.reshape(images, 1) == jnp.arange(classes)[None, :]).astype(F32)
        d_logits = ((soft_prob - onehot) / examples).astype(BF16)
        d_top = (dot_rhs_t(d_logits, w_head_b) / image).astype(BF16)
        d_hid_top = dot_rhs_t(d_top, w_out_b[layers - 1])
        d_hid_top = jnp.pad(d_hid_top, ((0, 8 - images), (0, 0))).reshape(8, chunks, CHUNK).transpose(1, 0, 2)

        hid_sum = hid_sum[:, :images].transpose(1, 0, 2).reshape(images, hidden)
        hid_high = lax.reduce_precision(hid_sum, 8, 7)
        hid_low = (hid_sum - hid_high).astype(BF16)
        wide = lambda a, b: jnp.concatenate([a, b]).reshape(2 * images, -1, LANES).transpose(1, 0, 2)
        logit_pad = jnp.pad(d_logits, ((0, 0), (0, 1024 - classes)))
        extra = jnp.concatenate([
            wide(hid_high.astype(BF16), hid_low),
            wide(d_top, d_top),
            wide(pooled, jnp.zeros_like(pooled)),
            wide(logit_pad, jnp.zeros_like(logit_pad)),
        ])

        total, images_all = backward(
            hid, slope, x_in, x_mid, w_in_b, w_out_b,
            jnp.pad(d_top.astype(F32), ((0, 8 - images), (0, 0))), d_hid_top, extra, image,
        )

        rates = jnp.stack([learn_rate, mom_coef])
        x_last = x_next.reshape(-1, dim)
        new_w_in, new_mom_in, new_w_out, new_mom_out, new_w_head, new_mom_head, logits_next = update_and_next(
            rates, x_last, w_in, mom_in, w_out, mom_out, total, images_all, w_head.T, mom_head.T, image
        )
        logits_next, new_w_head, new_mom_head = logits_next[: x_next.shape[0]], new_w_head.T, new_mom_head.T
        return (logits_next, new_w_in, new_w_out, new_w_head, new_mom_in, new_mom_out, new_mom_head)

    return jax.shard_map(
        local_step,
        mesh=mesh,
        in_specs=(P(None, "data", None, None), P(None, "data"), P("data", None, None), P(), P(), P(), P(), P(), P(), P(), P()),
        out_specs=(P("data", None), P(), P(), P(), P(), P(), P()),
        check_vma=False,
    )
```

time: 1490 us -> 587 us (0.39)
  matrix products: 688 us -> 6.55 us
  waiting for transfers between devices: 575 us -> 0 us
  Pallas kernels: 0 us -> 573 us
  other arithmetic: 188 us -> 3.09 us
  local copies, waits for them, and re-layouts: 17.6 us -> 2.15 us
  between operations: 17.3 us -> 2.04 us
    dot_general x59 -> x3, matrix products: 688 us -> 6.55 us  [the longest x2 4.01 us: dot_rhs_t(): lax.dot_general(a, b, (((1,), (1,)), ((), ())), preferred_element_type=F32)]
    psum x1 -> x0, waiting for transfers between devices: 575 us -> none  [local_step(): red_head = lax.psum(sum_head.astype(jnp.bfloat16), 'data')]
    pallas_call x0 -> x3, Pallas kernels: none -> 573 us  [the longest x1 328 us: backward(): pl.pallas_call(functools.partial(backward_kernel, tokens=tokens, image=im...]
    convert_element_type x7 -> x3, other arithmetic: 157 us -> 1 us  [the longest x1 0.89 us: local_step(): pooled = (top_sum[:images] / image).astype(BF16)]
    reduce_sum x21 -> x1, other arithmetic: 22.3 us -> 0.2 us  [local_step(): soft_prob = jax.nn.softmax(dot(pooled, w_head_b), axis=-1)]
    unnamed x216 -> x6, local copies, waits for them, and re-layouts: 16.9 us -> 0.02 us
  transfers between devices with their start and end apart: 1 -> 0, of which waited for: 1 -> 0; matrix products, arithmetic and copies ran while one was open for 0% -> 0% of each run, Pallas kernels for 0% -> 0%
where the time goes in v1:
time: 587 us
  Pallas kernels  573 us (98%)
  matrix products  6.55 us (1%)
    pallas_call x1, Pallas kernels, backward(): pl.pallas_call(functools.partial(backward_kernel, tokens=tokens, image=im...  328 us
    pallas_call x1, Pallas kernels, forward(): pl.pallas_call(functools.partial(forward_kernel, tokens=tokens, image=ima...  123 us
    pallas_call x1, Pallas kernels, update_and_next(): pl.pallas_call(functools.partial(update_kernel, tokens=tokens, image=imag...  122 us

profile of v1, /device:TPU:0, one launch (start us, length us, event | category | flops | bytes accessed | tf_op | source)
XLA Modules:
  0.0 587.0 jit_solution(15470039634414146841)
XLA Ops:
  0.6 0.0 copy-start.2
  0.6 123.4 %forward.1 = (bf16[4,6,2304,512]{3,2,1,0:T(8,128)(2,1)}, bf16[4,6,2304,512]{3,2,1,0:T(8,128)(2,1)}, bf16[4,768,3072]{2,1,0:T(8,128)(2,1)}, bf16[4,3072,768]{2,1,...) custom-call(bf16[2304,768]{1,0:T(8,128)(2,1)} %bitcast.36, ...), custom_call_target="tpu_custom_call" | custom-call | tf_op jit(solution)/shard_map/forward/pallas_call | solution.py:153
  124.1 0.0 copy-start
  124.1 0.0 copy-start.1
  124.1 0.9 multiply_convert_fusion.1
  125.0 2.5 fusion.9
  127.6 0.2 fusion.8
  127.8 0.0 copy-done.2
  127.8 0.1 eq.15
  127.9 0.1 multiply_convert_fusion
  128.0 0.0 copy-done
  128.0 0.4 fusion.3
  128.3 0.6 pad_maximum_fusion.1
  129.0 0.0 copy-done.1
  129.1 0.7 pad_maximum_fusion.extra
  129.7 3.6 fusion
  133.4 0.7 pad.18
  134.0 327.7 %backward.1 = (bf16[7,9216,256]{2,1,0:T(8,128)(2,1)}, bf16[22,256,256]{2,1,0:T(8,128)(2,1)}) custom-call(bf16[4,6,2304,512]{3,2,1,0:T(8,128)(2,1)} %get-tuple-element.23.hid, bf16[4,6,2304,512]{3,2,1,0:T(8,128)(2,1)} %get-tuple-element.24.slope, bf16[2304,768]{1,0:T(8,128)(2,1)} %bitcast.37, bf16[4,2304,768]{2,1,0:T(8,128)(2,1)} %get-tuple-element.25.x_mid, ...), custom_call_target="tpu_custom_call" | custom-call | tf_op jit(solution)/shard_map/backward/pallas_call | solution.py:504
  463.0 0.6 pad_maximum_fusion.2.rates
  463.6 122.0 %update_next.1 = (f32[4,768,3072]{2,1,0:T(8,128)}, f32[4,768,3072]{2,1,0:T(8,128)}, f32[4,3072,768]{2,1,0:T(8,128)}, f32[4,3072,768]{2,1,0:T(8,128)}, f32[1000,7...) custom-call(f32[2]{0:T(128)} %pad_maximum_fusion.2.rates, bf16[1152,768]{1,0:T(8,128)(2,1)} %bitcast.39, ...), custom_call_target="tpu_custom_call" | custom-call | tf_op jit(solution)/shard_map/update_next/pallas_call | solution.py:701
  585.6 1.4 slice.15
  (5 shorter events, 0.1 us)
Async XLA Ops:
  0.6 127.1 %copy-start.2 = (s32[2,2]{1,0:T(2,128)S(1)}, s32[2,2]{1,0:T(2,128)}, u32[]{:S(2)}) copy-start(s32[2,2]{1,0:T(2,128)} %param.12) | copy-start | bytes 52
  124.1 3.9 copy-start
  124.1 4.9 copy-start.1

commit v2 on v1

--- a/solution.py
+++ b/solution.py
@@ -195,7 +195,7 @@
 GATHER = (8, 9, 10, 12, 14, 15)
 TICKS = 24
 LAST_TICK = READY[1] + 3 * (PAIRS - 1) + GATHER[-1] + 1
-GROUPS = 22
+GROUPS = 11
 EXTRA_TICKS = {5: 2, 6: 5, 7: 8, 8: 11, 9: 15, 10: 19}
 
 
@@ -331,28 +331,33 @@
             for stream in range(2):
                 at(GATHER[step], stream, functools.partial(gather_step, step, stream))
 
-    def extra_rows(level):
+    def extra_rows(color, level):
         start, size = core * 16, 16
         for step in range(level):
             size = size // 2
-            start = start + bits[0][step] * size
-        return images_all.at[:, pl.ds(pl.multiple_of(start * 8, 8), size * 8)]
-
-    def extra_copy(stage):
-        spot = extra_rows(9 - stage)
-        mask = 1 if stage == 9 else MASKS[0][8 - stage]
-        src = extra if stage == 5 else spot
-        return remote(src, spot, extra_send.at[stage - 5], extra_recv.at[stage - 5], mask)
+            start = start + bits[color][step] * size
+        return images_all.at[color, :, pl.ds(pl.multiple_of(start * 8, 8), size * 8)]
+
+    def extra_copy(stage, color):
+        spot = extra_rows(color, 9 - stage)
+        mask = 1 if stage == 9 else MASKS[color][8 - stage]
+        src = extra.at[color] if stage == 5 else spot
+        at = (stage - 5, color)
+        return remote(src, spot, extra_send.at[at], extra_recv.at[at], mask)
+
+    def extra_own(color):
+        return pltpu.make_async_copy(extra.at[color], extra_rows(color, 4), extra_local.at[color])
 
     def exchange_extra(stage):
-        if stage > 5:
-            extra_copy(stage - 1).wait()
-        if stage == 6:
-            pltpu.make_async_copy(extra, extra_rows(4), extra_local).wait()
-        if stage == 5:
-            pltpu.make_async_copy(extra, extra_rows(4), extra_local).start()
-        if stage <= 9:
-            extra_copy(stage).start()
+        for color in range(2):
+            if stage > 5:
+                extra_copy(stage - 1, color).wait()
+            if stage == 6:
+                extra_own(color).wait()
+            if stage == 5:
+                extra_own(color).start()
+            if stage <= 9:
+                extra_copy(stage, color).start()
 
     def run_extra(tick, ticks):
         for stage, when in EXTRA_TICKS.items():
@@ -507,7 +512,7 @@
         out_specs=[hbm, hbm],
         out_shape=[
             jax.ShapeDtypeStruct((PAIRS, 2 * STREAM, LANES), BF16),
-            jax.ShapeDtypeStruct((GROUPS, 256, LANES), BF16),
+            jax.ShapeDtypeStruct((2, GROUPS, 256, LANES), BF16),
         ],
         scratch_shapes=[
             pltpu.VMEM((2, 2 * STREAM, LANES), BF16),
@@ -528,9 +533,9 @@
             dma((10, 2, 2, 2)),
             dma((10, 2, 2, 2)),
             dma((2, 2, 2)),
-            dma((5,)),
-            dma((5,)),
-            dma,
+            dma((5, 2)),
+            dma((5, 2)),
+            dma((2,)),
         ],
         compiler_params=pltpu.CompilerParams(vmem_limit_bytes=VMEM_LIMIT, collective_id=0, has_side_effects=True),
         name="backward",
@@ -543,8 +548,8 @@
 def update_kernel(
     rates, x_hbm, w_in, m_in, w_out, m_out, grads, images_all, w_head, m_head,
     new_w_in, new_m_in, new_w_out, new_m_out, new_w_head, new_m_head, next_logits,
-    b_w_in, b_m_in, b_w_out, b_m_out, b_g_in, b_g_out, rows_all, x, n, acc, pre, hid, w_in_b, w_out_b,
-    load_sem, store_sem, x_sem, rows_sem, *, tokens, image, tile, chunks, layers,
+    b_w_in, b_m_in, b_w_out, b_m_out, b_g_in, b_g_out, rows_all, tops, b_head, x, n, acc, pre, hid, w_in_b, w_out_b,
+    load_sem, store_sem, x_sem, rows_sem, head_sem, *, tokens, image, tile, chunks, layers,
 ):
     rate, coef = rates[0], rates[1]
     steps = layers * chunks
@@ -586,6 +591,10 @@
         for load in loads(ahead):
             load.start()
     load_rows.start()
+    head_loads = [pltpu.make_async_copy(src, b_head.at[i], head_sem.at[i]) for i, src in enumerate((w_head, m_head))]
+    head_stores = [pltpu.make_async_copy(b_head.at[i], dst, head_sem.at[i]) for i, dst in enumerate((new_w_head, new_m_head))]
+    for load in head_loads:
+        load.start()
     load_x.wait()
 
     def start(rows):
@@ -594,16 +603,27 @@
 
     row_loop(tokens, 128, start)
 
-    load_rows.wait()
-    classes = w_head.shape[0]
-    for group in range(0, classes, LANES):
-        size = min(LANES, classes - group)
-        for part in range(3):
-            at = (slice(group, group + size), span(part, LANES))
-            grad = dot_lhs_t(rows_all[18 + group // LANES], rows_all[15 + part])[:size]
-            moment = coef * m_head[at] + grad
-            new_m_head[at] = moment
-            new_w_head[at] = w_head[at] - rate * moment
+    def per_image():
+        load_rows.wait()
+        for load in head_loads:
+            load.wait()
+        low = lax.broadcasted_iota(jnp.int32, (256, LANES), 0) % 8 >= 4
+        for color in range(2):
+            for third in range(3):
+                value = rows_all[color, 6 + third].astype(F32)
+                tops[color, third] = jnp.where(low, pltpu.roll(value, 4, 0), value).astype(BF16)
+        classes = w_head.shape[0]
+        for group in range(4):
+            start = group * LANES
+            size = min(LANES, classes - start)
+            for third in range(3):
+                at = (slice(start, start + size), span(third, LANES))
+                grad = dot_lhs_t(rows_all[group // 2, 9 + group % 2], rows_all[group // 2, 6 + third])[:size]
+                moment = coef * b_head[(1, *at)] + grad
+                b_head[(1, *at)] = moment
+                b_head[(0, *at)] = b_head[(0, *at)] - rate * moment
+        for store in head_stores:
+            store.start()
 
     @pl.loop(0, steps)
     def _(step):
@@ -628,6 +648,10 @@
                 b_w_out[slot, :, cols] = weight
                 w_out_b[:, cols] = weight.astype(BF16)
 
+        @pl.when(step == 2)
+        def _():
+            per_image()
+
         @pl.when(layer < layers - 1)
         def _():
             update_out(lambda third: b_g_out[slot, span(third, CHUNK), :].astype(F32))
@@ -635,7 +659,8 @@
         @pl.when(layer == layers - 1)
         def _():
             def top_grad(third):
-                parts = [dot_lhs_t(rows_all[2 * chunk + half], rows_all[12 + third]) for half in range(2)]
+                color = chunk // 3
+                parts = [dot_lhs_t(rows_all[color, 2 * (chunk % 3) + half], tops[color, third]) for half in range(2)]
                 return jnp.concatenate(parts, axis=0)
 
             update_out(top_grad)
@@ -685,7 +710,9 @@
             row_loop(tokens, 128, finish)
 
     pooled = (image_sums(x[...], image) / image).astype(BF16)
-    next_logits[...] = dot_rhs_t(pooled, new_w_head[...].astype(BF16))
+    next_logits[...] = dot_rhs_t(pooled, b_head[0].astype(BF16))
+    for store in head_stores:
+        store.wait()
     for store in stores(steps - 1):
         store.wait()
 
@@ -700,8 +727,8 @@
     dma = pltpu.SemaphoreType.DMA
     return pl.pallas_call(
         functools.partial(update_kernel, tokens=tokens, image=image, tile=tile, chunks=chunks, layers=layers),
-        in_specs=[pl.BlockSpec(memory_space=pltpu.SMEM)] + [hbm] * 7 + [vmem] * 2,
-        out_specs=[hbm] * 4 + [vmem] * 3,
+        in_specs=[pl.BlockSpec(memory_space=pltpu.SMEM)] + [hbm] * 9,
+        out_specs=[hbm] * 6 + [vmem],
         out_shape=[
             jax.ShapeDtypeStruct(w_in.shape, F32),
             jax.ShapeDtypeStruct(w_in.shape, F32),
@@ -718,7 +745,9 @@
             pltpu.VMEM((SLOTS, CHUNK, dim), F32),
             pltpu.VMEM((SLOTS, 1536, LANES), BF16),
             pltpu.VMEM((SLOTS, 1536, LANES), BF16),
-            pltpu.VMEM((GROUPS, 256, LANES), BF16),
+            pltpu.VMEM((2, GROUPS, 256, LANES), BF16),
+            pltpu.VMEM((2, 3, 256, LANES), BF16),
+            pltpu.VMEM((2, *w_head.shape), F32),
             pltpu.VMEM((tokens, dim), BF16),
             pltpu.VMEM((tokens, dim), BF16),
             pltpu.VMEM((tokens, dim), F32),
@@ -730,6 +759,7 @@
             dma((SLOTS, 4)),
             dma,
             dma,
+            dma((2,)),
         ],
         compiler_params=pltpu.CompilerParams(vmem_limit_bytes=VMEM_LIMIT),
         name="update_next",
@@ -764,12 +794,10 @@
         hid_low = (hid_sum - hid_high).astype(BF16)
         wide = lambda a, b: jnp.concatenate([a, b]).reshape(2 * images, -1, LANES).transpose(1, 0, 2)
         logit_pad = jnp.pad(d_logits, ((0, 0), (0, 1024 - classes)))
-        extra = jnp.concatenate([
-            wide(hid_high.astype(BF16), hid_low),
-            wide(d_top, d_top),
-            wide(pooled, jnp.zeros_like(pooled)),
-            wide(logit_pad, jnp.zeros_like(logit_pad)),
-        ])
+        sums = wide(hid_high.astype(BF16), hid_low).reshape(2, -1, 2 * images, LANES)
+        tops = jnp.broadcast_to(wide(d_top, pooled)[None], (2, 3, 2 * images, LANES))
+        logit_rows = wide(jnp.zeros_like(logit_pad), logit_pad).reshape(2, -1, 2 * images, LANES)
+        extra = jnp.concatenate([sums, tops, logit_rows], axis=1)
 
         total, images_all = backward(
             hid, slope, x_in, x_mid, w_in_b, w_out_b,

time: 587 us -> 586 us (level)
  no operation moved by 1% of the time
where the time goes in v2:
time: 586 us
  Pallas kernels  572 us (98%)
  matrix products  6.55 us (1%)
    pallas_call x1, Pallas kernels, backward(): pl.pallas_call(functools.partial(backward_kernel, tokens=tokens, image=im...  328 us
    pallas_call x1, Pallas kernels, forward(): pl.pallas_call(functools.partial(forward_kernel, tokens=tokens, image=ima...  123 us
    pallas_call x1, Pallas kernels, update_and_next(): pl.pallas_call(functools.partial(update_kernel, tokens=tokens, image=imag...  121 us

profile of v2, /device:TPU:0, one launch (start us, length us, event | category | flops | bytes accessed | tf_op | source)
XLA Modules:
  0.0 585.7 jit_solution(8608636071858732992)
XLA Ops:
  0.6 0.0 copy-start.2
  0.6 123.4 %forward.1 = (bf16[4,6,2304,512]{3,2,1,0:T(8,128)(2,1)}, bf16[4,6,2304,512]{3,2,1,0:T(8,128)(2,1)}, bf16[4,768,3072]{2,1,0:T(8,128)(2,1)}, bf16[4,3072,768]{2,1,...) custom-call(bf16[2304,768]{1,0:T(8,128)(2,1)} %bitcast.36, ...), custom_call_target="tpu_custom_call" | custom-call | tf_op jit(solution)/shard_map/forward/pallas_call | solution.py:153
  124.1 0.0 copy-start
  124.1 0.0 copy-start.1
  124.1 0.9 multiply_convert_fusion.1
  125.0 2.5 fusion.9
  127.6 0.2 fusion.8
  127.8 0.0 copy-done.2
  127.8 0.1 eq.15
  127.9 0.1 multiply_convert_fusion
  128.0 0.0 copy-done
  128.0 0.4 fusion.3
  128.3 0.6 pad_maximum_fusion.2
  129.0 0.0 copy-done.1
  129.1 0.7 pad_maximum_fusion.extra
  129.7 3.6 fusion
  133.4 0.7 pad.17
  134.0 327.9 %backward.1 = (bf16[7,9216,256]{2,1,0:T(8,128)(2,1)}, bf16[2,11,256,256]{3,2,1,0:T(8,128)(2,1)}) custom-call(bf16[4,6,2304,512]{3,2,1,0:T(8,128)(2,1)} %get-tuple-element.23.hid, bf16[4,6,2304,512]{3,2,1,0:T(8,128)(2,1)} %get-tuple-element.24.slope, bf16[2304,768]{1,0:T(8,128)(2,1)} %bitcast.37, bf16[4,2304,768]{2,1,0:T(8,128)(2,1)} %get-tuple-element.25.x_mid, ...), custom_call_target="tpu_custom_call" | custom-call | tf_op jit(solution)/shard_map/backward/pallas_call | solution.py:509
  463.2 0.6 pad_maximum_fusion.3.rates
  463.8 120.5 %update_next.1 = (f32[4,768,3072]{2,1,0:T(8,128)}, f32[4,768,3072]{2,1,0:T(8,128)}, f32[4,3072,768]{2,1,0:T(8,128)}, f32[4,3072,768]{2,1,0:T(8,128)}, f32[1000,7...) custom-call(f32[2]{0:T(128)} %pad_maximum_fusion.3.rates, bf16[1152,768]{1,0:T(8,128)(2,1)} %bitcast.39, ...), custom_call_target="tpu_custom_call" | custom-call | tf_op jit(solution)/shard_map/update_next/pallas_call | solution.py:728
  584.3 1.4 slice.15
  (5 shorter events, 0.1 us)
Async XLA Ops:
  0.6 127.1 %copy-start.2 = (s32[2,2]{1,0:T(2,128)S(1)}, s32[2,2]{1,0:T(2,128)}, u32[]{:S(2)}) copy-start(s32[2,2]{1,0:T(2,128)} %param.12) | copy-start | bytes 52
  124.1 3.9 copy-start
  124.1 4.9 copy-start.1
